TPU v7x, 512 devices: a whole 4x8x8 slice. The times are simulated.
512 devices in a mesh: kgrp: 128 (over y, x, z_hi), img: 4 (over z_lo, core).
Axes of the slice: x: 4, y: 8, z: 8 (z_hi: 4, z_lo: 2; z = z_hi * 2 + z_lo), core: 2. Of those that a mesh axis runs over, the one named last changes fastest.
Arguments:
- vectors: float32 [2, 16, 16384], P(None, 'img', 'kgrp'), may hold values from -6 to 6
- conduction: bfloat16 [256, 2, 8, 4, 4096], P('kgrp', None, None, 'img'), may hold values from -6 to 6
- valence: bfloat16 [256, 2, 8, 4, 4096], P('kgrp', None, None, 'img'), may hold values from -6 to 6
- hole_point: int32 [1], replicated, may hold values from 0 to 16383
- kpoint_grid: int32 [3, 256], replicated, may hold values from 0 to 11
- image_cells: int32 [3, 512], replicated, may hold values from -6 to 6
Outputs:
- psi_real: float32 [16, 4, 4096, 512], P(None, 'img', 'kgrp')
- psi_imag: float32 [16, 4, 4096, 512], P(None, 'img', 'kgrp')
All inputs are finite; a program needn't handle non-finite values.
Results may differ from a plain program's by a relative error of at most 0.0043.
Values may be sent and summed in bfloat16 or wider, within the bound.
A program may use at most 64 MiB of HBM per device.

v0:
```python
import jax
import jax.numpy as jnp
import numpy as np
from jax import lax
from jax.sharding import PartitionSpec as P

NV = 8
NC = 8
cosine_levels = np.cos(2.0 * np.pi * np.arange(12) / 12.0)
sine_levels = np.sin(2.0 * np.pi * np.arange(12) / 12.0)


def phase_table(kpoint_grid, image_cells):
    turn_count = kpoint_grid[0][:, None] * image_cells[0][None, :]
    turn_count = turn_count + kpoint_grid[1][:, None] * image_cells[1][None, :]
    turn_count = turn_count + kpoint_grid[2][:, None] * image_cells[2][None, :]
    turn_count = jnp.mod(turn_count, 12)
    cosine = jnp.zeros(turn_count.shape, jnp.float32)
    sine_part = jnp.zeros(turn_count.shape, jnp.float32)
    for level_index in range(12):
        matches = turn_count == level_index
        cosine = jnp.where(matches, jnp.float32(cosine_levels[level_index]), cosine)
        sine_part = jnp.where(matches, jnp.float32(sine_levels[level_index]), sine_part)
    upper_half = jnp.stack([cosine, sine_part], 1)
    lower_half = jnp.stack([-sine_part, cosine], 1)
    return jnp.stack([upper_half, lower_half], 0).astype(jnp.bfloat16)


def hole_weights(amplitudes, hole_values):
    norm_factor = (NV * NC) ** (-0.5)
    real_amplitude = amplitudes[0]
    imaginary_amplitude = amplitudes[1]
    real_hole = hole_values[:, 0]
    imaginary_hole = hole_values[:, 1]
    highest = lax.Precision.HIGHEST
    weight_real = jnp.einsum("skvc,kv->ksc", real_amplitude, real_hole, precision=highest)
    weight_real = weight_real + jnp.einsum(
        "skvc,kv->ksc", imaginary_amplitude, imaginary_hole, precision=highest
    )
    weight_imaginary = jnp.einsum("skvc,kv->ksc", imaginary_amplitude, real_hole, precision=highest)
    weight_imaginary = weight_imaginary - jnp.einsum(
        "skvc,kv->ksc", real_amplitude, imaginary_hole, precision=highest
    )
    return jnp.stack([weight_real * norm_factor, weight_imaginary * norm_factor], 1).astype(
        jnp.bfloat16
    )


def mixing(weights):
    weight_real = weights[:, 0]
    weight_imaginary = weights[:, 1]
    first_row = jnp.stack([weight_real, -weight_imaginary], 2)
    second_row = jnp.stack([weight_imaginary, weight_real], 2)
    return jnp.stack([first_row, second_row], 1)


def shards(vectors, conduction, valence, hole_point, kpoint_grid, image_cells):
    group_size = lax.axis_size("kgrp")
    local_k = conduction.shape[0]
    slab_width = conduction.shape[4]
    own_excitons = vectors.shape[1]
    blocks = vectors.shape[2] // group_size
    columns = vectors.reshape(2, own_excitons, group_size, blocks)
    owned_columns = lax.all_to_all(columns, "kgrp", split_axis=2, concat_axis=2, tiled=True)
    owned_columns = owned_columns.reshape(2, own_excitons, local_k, NV, NC)
    hole_offset = hole_point[0] % slab_width
    hole_slab = hole_point[0] // slab_width
    present = (lax.axis_index("img") == hole_slab).astype(jnp.float32)
    picked = (
        lax.dynamic_slice_in_dim(valence[:, :, :, 0, :], hole_offset, 1, 3)[..., 0].astype(
            jnp.float32
        )
        * present
    )
    hole_values = lax.psum(picked, "img")
    all_columns = lax.all_gather(owned_columns, "img", axis=1, tiled=True)
    weights = hole_weights(all_columns, hole_values)
    phases = phase_table(kpoint_grid, image_cells)
    products = jnp.einsum(
        "kasbc,kbcp->sakp",
        mixing(weights),
        conduction[:, :, :, 0, :],
        preferred_element_type=jnp.float32,
    ).astype(jnp.bfloat16)
    summed = jnp.einsum(
        "sakp,akbn->spbn",
        lax.all_to_all(products, "kgrp", split_axis=3, concat_axis=2, tiled=True),
        phases,
        preferred_element_type=jnp.float32,
    )
    normal_scale = (2 * kpoint_grid.shape[1]) ** (-0.5)
    summed = summed * normal_scale
    return (summed[:, None, :, 0, :], summed[:, None, :, 1, :])


def solution(mesh):
    placed = (
        P(None, "img", "kgrp"),
        P("kgrp", None, None, "img", None),
        P("kgrp", None, None, "img", None),
        P(),
        P(),
        P(),
    )
    return jax.shard_map(
        shards,
        mesh=mesh,
        in_specs=placed,
        out_specs=(P(None, "img", "kgrp", None), P(None, "img", "kgrp", None)),
        check_vma=False,
    )
```

profile of v0, /device:TPU:8, one launch (start us, length us, event | category | flops | bytes accessed | tf_op | source)
XLA Modules:
  0.0 111.9 jit_solution(5236022632202495821)
XLA Ops:
  0.6 0.0 copy-start
  0.6 1.5 %copy.29 = f32[2,4,128]{1,0,2:T(2,128)} copy(f32[2,4,128]{2,1,0:T(4,128)} %param.6) | data formatting | bytes 8192 | tf_op args[0]
  2.2 19.8 %all-to-all-start = ((f32[2,4,128,1]{1,0,3,2:T(2,128)}), f32[2,4,128,1]{1,0,3,2:T(2,128)S(1)}, u32[]{:S(2)}, u32[]{:S(2)}) async-start(f32[2,4,128,1]{1,0,3,2:T(2,128)} %bitcast.4), calls=%async_computation | async-start | bytes 262144 | tf_op jit(solution)/shard_map/all_to_all | solution.py:64
  22.7 0.9 multiply_reduce_fusion
  23.5 6.3 %psum.7 = f32[2,2,8]{2,1,0:T(2,128)S(1)} all-reduce(f32[2,2,8]{2,1,0:T(2,128)S(1)} %multiply_reduce_fusion), channel_id=1, replica_groups=mesh['kgrp'=128,'img'=4] {'img'}, use_global_device_ids=true, to_apply=%region_0.1 | all-reduce | flops 32 | bytes 256 | tf_op jit(solution)/shard_map/psum | solution.py:75
  29.9 6.6 %all-to-all-done = f32[2,4,128,1]{1,0,3,2:T(2,128)S(1)} async-done(((f32[2,4,128,1]{1,0,3,2:T(2,128)}), f32[2,4,128,1]{1,0,3,2:T(2,128)S(1)}, u32[]{:S(2)}, u32[]{:S(2)}) %all-to-all-start) | async-done | bytes 4128 | tf_op jit(solution)/shard_map/all_to_all | solution.py:64
  36.5 0.3 copy.30
  36.8 5.8 %all_gather.3 = f32[2,16,2,8,8]{4,3,2,0,1:T(8,128)S(1)} all-gather(f32[2,4,2,8,8]{4,3,2,0,1:T(8,128)S(1)} %copy.30), channel_id=1, replica_groups=mesh['kgrp'=128,'img'=4] {'img'}, dimensions={1}, use_global_device_ids=true | all-gather | bytes 20480 | tf_op jit(solution)/shard_map/all_gather | solution.py:76
  42.6 0.3 fusion.15
  42.8 0.3 fusion.13
  43.1 0.3 fusion.19
  43.4 0.3 fusion.17
  43.6 0.1 copy.41
  43.7 0.1 copy.44
  43.8 0.1 copy.45
  43.8 0.1 copy.46
  43.9 0.0 copy-done
  43.9 0.3 fusion.1
  44.3 7.1 %copy.32 = bf16[16,2,2,4096]{0,1,2,3:T(2,128)(2,1)} copy(bf16[16,2,2,4096]{3,0,1,2:T(8,128)(2,1)S(1)} %fusion.1) | data formatting | bytes 1048576 | tf_op jit(solution)/shard_map/convert_element_type | solution.py:84
  51.4 0.0 copy-start.2
  51.4 0.0 copy-start.1
  51.4 12.9 %reshape.653 = bf16[128,2,1024]{2,1,0:T(2,128)(2,1)} reshape(bf16[4096,2,2,16]{3,2,1,0:T(2,128)(2,1)} %bitcast.114) | data formatting | bytes 1048576
  64.3 9.2 %all-to-all-start.1 = ((bf16[128,2,1024]{2,1,0:T(2,128)(2,1)}), bf16[128,2,1024]{2,1,0:T(2,128)(2,1)S(1)}, u32[]{:S(2)}, u32[]{:S(2)}) async-start(bf16[128,2,1024]{2,1,0:T(2,128)(2,1)} %reshape.653), calls=%async_computation.1 | async-start | bytes 1048576 | tf_op jit(solution)/shard_map/all_to_all | solution.py:87
  73.5 0.0 copy-done.2
  73.6 0.0 copy-done.1
  73.6 1.1 fusion.12
  74.6 0.1 maximum_bitcast_fusion.2
  74.7 22.0 %all-to-all-done.1 = bf16[128,2,1024]{2,1,0:T(2,128)(2,1)S(1)} async-done(((bf16[128,2,1024]{2,1,0:T(2,128)(2,1)}), bf16[128,2,1024]{2,1,0:T(2,128)(2,1)S(1)}, u32[]{:S(2)}, u32[]{:S(2)}) %all-to-all-start.1) | async-done | bytes 524320 | tf_op jit(solution)/shard_map/all_to_all | solution.py:87
  96.8 4.1 %reshape.654 = bf16[4096,2,2,16]{3,2,1,0:T(2,128)(2,1)} reshape(bf16[128,2,1024]{2,1,0:T(2,128)(2,1)S(1)} %all-to-all-done.1) | data formatting | bytes 1048576
  100.9 8.6 %copy.52 = bf16[16,2,2,128,32]{4,0,2,3,1:T(8,128)(2,1)S(1)} copy(bf16[16,2,2,128,32]{0,1,2,4,3:T(2,128)(2,1)} %bitcast.115) | data formatting | bytes 1048576 | tf_op jit(solution)/shard_map/all_to_all | solution.py:87
  109.5 1.0 bitcast_multiply_fusion
  110.4 1.5 %slice_bitcast_fusion = (f32[16,1,32,512]{3,2,1,0:T(8,128)}, f32[16,1,32,512]{3,2,1,0:T(8,128)}) fusion(f32[16,32,2,512]{3,1,2,0:T(8,128)S(1)} %bitcast_multiply_fusion), kind=kLoop, calls=%fused_computation.6 | loop fusion | bytes 4194304
  (6 shorter events, 0.1 us)
Async XLA Ops:
  0.6 43.3 %copy-start = (bf16[2,2,8,1,4096]{4,2,3,1,0:T(8,128)(2,1)S(1)}, bf16[2,2,8,1,4096]{4,2,3,1,0:T(8,128)(2,1)}, u32[]{:S(2)}) copy-start(bf16[2,2,8,1,4096]{4,2,3,1,0:T(8,128)(2,1)} %param.7) | copy-start | bytes 786436
  2.2 34.3 %all-to-all-start = ((f32[2,4,128,1]{1,0,3,2:T(2,128)}), f32[2,4,128,1]{1,0,3,2:T(2,128)S(1)}, u32[]{:S(2)}, u32[]{:S(2)}) async-start(f32[2,4,128,1]{1,0,3,2:T(2,128)} %bitcast.4), calls=%async_computation | async-start | bytes 262144 | tf_op jit(solution)/shard_map/all_to_all | solution.py:64
  51.4 22.1 %copy-start.2 = (s32[3,256]{1,0:T(4,128)S(1)}, s32[3,256]{1,0:T(4,128)}, u32[]{:S(2)}) copy-start(s32[3,256]{1,0:T(4,128)} %param.10) | copy-start | bytes 9220
  51.4 22.1 %copy-start.1 = (s32[3,512]{1,0:T(4,128)S(1)}, s32[3,512]{1,0:T(4,128)}, u32[]{:S(2)}) copy-start(s32[3,512]{1,0:T(4,128)} %param.11) | copy-start | bytes 18436
  64.3 32.4 %all-to-all-start.1 = ((bf16[128,2,1024]{2,1,0:T(2,128)(2,1)}), bf16[128,2,1024]{2,1,0:T(2,128)(2,1)S(1)}, u32[]{:S(2)}, u32[]{:S(2)}) async-start(bf16[128,2,1024]{2,1,0:T(2,128)(2,1)} %reshape.653), calls=%async_computation.1 | async-start | bytes 1048576 | tf_op jit(solution)/shard_map/all_to_all | solution.py:87
where the time goes:
time: 112 us
  local copies, waits for them, and re-layouts  36.4 us (32%)
  starting transfers between devices  29 us (26%)
  waiting for transfers between devices  28.6 us (26%)
  blocking collectives  12.1 us (11%)
  matrix products  2.31 us (2%)
  other arithmetic  2.02 us (2%)
  between operations  1.47 us (1%)
    all_to_all x1, waiting for transfers between devices, shards(): lax.all_to_all(products, 'kgrp', split_axis=3, concat_axis=2, tiled=True)  22 us
    unnamed x10, local copies, waits for them, and re-layouts  20.1 us
    all_to_all x1, starting transfers between devices, shards(): lax.all_to_all(columns, 'kgrp', split_axis=2, concat_axis=2, tiled=True)  19.8 us
    all_to_all x1, starting transfers between devices, shards(): lax.all_to_all(products, 'kgrp', split_axis=3, concat_axis=2, tiled=True)  9.2 us
    all_to_all x1, local copies, waits for them, and re-layouts, shards(): lax.all_to_all(products, 'kgrp', split_axis=3, concat_axis=2, tiled=True)  8.56 us
    convert_element_type x1, local copies, waits for them, and re-layouts, shards(): products = jnp.einsum('kasbc,kbcp->sakp', mixing(weights), conduction[:,...  7.13 us
    all_to_all x1, waiting for transfers between devices, shards(): lax.all_to_all(columns, 'kgrp', split_axis=2, concat_axis=2, tiled=True)  6.61 us
    psum x1, blocking collectives, shards(): hole_values = lax.psum(picked, 'img')  6.33 us
  transfers between devices with their start and end apart: 2, of which 2 were waited for; matrix products, arithmetic and copies ran while one was open for 2% of the time, Pallas kernels for 0%

commit v1 on v0

--- a/solution.py
+++ b/solution.py
@@ -73,7 +73,9 @@
         * present
     )
     hole_values = lax.psum(picked, "img")
-    all_columns = lax.all_gather(owned_columns, "img", axis=1, tiled=True)
+    near = jnp.stack([owned_columns for _ in range(lax.axis_size("img"))], 0)
+    frame_out = lax.all_to_all(near, "img", 0, 0)
+    all_columns = jnp.concatenate(frame_out, axis=1)
     weights = hole_weights(all_columns, hole_values)
     phases = phase_table(kpoint_grid, image_cells)
     products = jnp.einsum(

time: 112 us -> 116 us (1.036)
  the two profiles are of different devices: /device:TPU:8 before, /device:TPU:64 now
where the time goes in v1:
time: 116 us; the launch traced here: 115 us
  blocking collectives  39.7 us (34%)
  local copies, waits for them, and re-layouts  37.2 us (32%)
  waiting for transfers between devices  21.9 us (19%)
  starting transfers between devices  10.1 us (9%)
  other arithmetic  2.71 us (2%)
  matrix products  2.3 us (2%)
  between operations  1.5 us (1%)
    all_to_all x1, blocking collectives, shards(): lax.all_to_all(columns, 'kgrp', split_axis=2, concat_axis=2, tiled=True)  34 us
    all_to_all x1, waiting for transfers between devices, shards(): lax.all_to_all(products, 'kgrp', split_axis=3, concat_axis=2, tiled=True)  21.9 us
    unnamed x12, local copies, waits for them, and re-layouts  20.4 us
    all_to_all x1, local copies, waits for them, and re-layouts, shards(): lax.all_to_all(products, 'kgrp', split_axis=3, concat_axis=2, tiled=True)  8.56 us
    convert_element_type x1, local copies, waits for them, and re-layouts, shards(): products = jnp.einsum('kasbc,kbcp->sakp', mixing(weights), conduction[:,...  7.14 us
    all_to_all x1, starting transfers between devices, shards(): lax.all_to_all(products, 'kgrp', split_axis=3, concat_axis=2, tiled=True)  6.36 us
    psum x1, blocking collectives, shards(): hole_values = lax.psum(picked, 'img')  5.75 us
    all_to_all x1, starting transfers between devices, shards(): frame_out = lax.all_to_all(near, 'img', 0, 0)  3.78 us
  transfers between devices with their start and end apart: 2, of which 1 were waited for; matrix products, arithmetic and copies ran while one was open for 2% of the time, Pallas kernels for 0%

profile of v1, /device:TPU:64, one launch (start us, length us, event | category | flops | bytes accessed | tf_op | source)
XLA Modules:
  0.0 115.5 jit_solution(3595970362202070796)
XLA Ops:
  0.6 0.0 copy-start
  0.6 0.9 copy.20
  1.5 34.0 %all_to_all.28 = f32[2,4,128,1]{1,0,3,2:T(2,128)S(1)} all-to-all(f32[2,4,128,1]{1,0,3,2:T(2,128)S(1)} %bitcast.122), channel_id=1, replica_groups=mesh['kgrp'=128,'img'=4] {'kgrp'}, dimensions={2} | all-to-all | bytes 8192 | tf_op jit(solution)/shard_map/all_to_all | solution.py:64
  35.5 0.3 copy.21
  35.8 0.8 reshape.660
  36.6 3.8 %all-to-all-start.1 = ((f32[4,1,1024]{2,1,0:T(1,128)}), f32[4,1,1024]{2,1,0:T(1,128)S(1)}, u32[]{:S(2)}, u32[]{:S(2)}) async-start(f32[4,1,1024]{2,1,0:T(1,128)} %reshape.660), calls=%async_computation.1 | async-start | bytes 32768 | tf_op jit(solution)/shard_map/all_to_all | solution.py:77
  41.0 0.9 multiply_reduce_fusion
  41.9 5.8 %psum.7 = f32[2,2,8]{2,1,0:T(2,128)S(1)} all-reduce(f32[2,2,8]{2,1,0:T(2,128)S(1)} %multiply_reduce_fusion), channel_id=1, replica_groups=mesh['kgrp'=128,'img'=4] {'img'}, use_global_device_ids=true, to_apply=%region_0.1 | all-reduce | flops 32 | bytes 256 | tf_op jit(solution)/shard_map/psum | solution.py:75
  47.6 0.0 all-to-all-done.1
  47.6 0.5 broadcast.741
  48.2 0.7 reduce.2
  48.9 0.2 reshape.661
  49.1 0.3 fusion.15
  49.3 0.3 fusion.13
  49.6 0.3 fusion.19
  49.8 0.3 fusion.17
  50.1 0.1 copy.32
  50.2 0.1 copy.35
  50.2 0.1 copy.36
  50.3 0.1 copy.37
  50.4 0.0 copy-done
  50.4 0.3 fusion.1
  50.8 7.1 %copy.23 = bf16[16,2,2,4096]{0,1,2,3:T(2,128)(2,1)} copy(bf16[16,2,2,4096]{3,0,1,2:T(8,128)(2,1)S(1)} %fusion.1) | data formatting | bytes 1048576 | tf_op jit(solution)/shard_map/convert_element_type | solution.py:86
  57.9 0.0 copy-start.2
  57.9 0.0 copy-start.1
  57.9 12.9 %reshape.662 = bf16[128,2,1024]{2,1,0:T(2,128)(2,1)} reshape(bf16[4096,2,2,16]{3,2,1,0:T(2,128)(2,1)} %bitcast.113) | data formatting | bytes 1048576
  70.8 6.4 %all-to-all-start.2 = ((bf16[128,2,1024]{2,1,0:T(2,128)(2,1)}), bf16[128,2,1024]{2,1,0:T(2,128)(2,1)S(1)}, u32[]{:S(2)}, u32[]{:S(2)}) async-start(bf16[128,2,1024]{2,1,0:T(2,128)(2,1)} %reshape.662), calls=%async_computation.2 | async-start | bytes 1048576 | tf_op jit(solution)/shard_map/all_to_all | solution.py:89
  77.2 0.0 copy-done.2
  77.2 0.0 copy-done.1
  77.2 1.1 fusion.12
  78.3 0.1 maximum_bitcast_fusion.2
  78.4 21.9 %all-to-all-done.2 = bf16[128,2,1024]{2,1,0:T(2,128)(2,1)S(1)} async-done(((bf16[128,2,1024]{2,1,0:T(2,128)(2,1)}), bf16[128,2,1024]{2,1,0:T(2,128)(2,1)S(1)}, u32[]{:S(2)}, u32[]{:S(2)}) %all-to-all-start.2) | async-done | bytes 524320 | tf_op jit(solution)/shard_map/all_to_all | solution.py:89
  100.3 4.1 %reshape.663 = bf16[4096,2,2,16]{3,2,1,0:T(2,128)(2,1)} reshape(bf16[128,2,1024]{2,1,0:T(2,128)(2,1)S(1)} %all-to-all-done.2) | data formatting | bytes 1048576
  104.5 8.6 %copy.43 = bf16[16,2,2,128,32]{4,0,2,3,1:T(8,128)(2,1)S(1)} copy(bf16[16,2,2,128,32]{0,1,2,4,3:T(2,128)(2,1)} %bitcast.114) | data formatting | bytes 1048576 | tf_op jit(solution)/shard_map/all_to_all | solution.py:89
  113.0 0.9 bitcast_multiply_fusion
  114.0 1.5 %slice_bitcast_fusion = (f32[16,1,32,512]{3,2,1,0:T(8,128)}, f32[16,1,32,512]{3,2,1,0:T(8,128)}) fusion(f32[16,32,2,512]{3,1,2,0:T(8,128)S(1)} %bitcast_multiply_fusion), kind=kLoop, calls=%fused_computation.6 | loop fusion | bytes 4194304
  (7 shorter events, 0.1 us)
Async XLA Ops:
  0.6 49.8 %copy-start = (bf16[2,2,8,1,4096]{4,2,3,1,0:T(8,128)(2,1)S(1)}, bf16[2,2,8,1,4096]{4,2,3,1,0:T(8,128)(2,1)}, u32[]{:S(2)}) copy-start(bf16[2,2,8,1,4096]{4,2,3,1,0:T(8,128)(2,1)} %param.7) | copy-start | bytes 786436
  36.6 11.1 %all-to-all-start.1 = ((f32[4,1,1024]{2,1,0:T(1,128)}), f32[4,1,1024]{2,1,0:T(1,128)S(1)}, u32[]{:S(2)}, u32[]{:S(2)}) async-start(f32[4,1,1024]{2,1,0:T(1,128)} %reshape.660), calls=%async_computation.1 | async-start | bytes 32768 | tf_op jit(solution)/shard_map/all_to_all | solution.py:77
  57.9 19.3 %copy-start.2 = (s32[3,256]{1,0:T(4,128)S(1)}, s32[3,256]{1,0:T(4,128)}, u32[]{:S(2)}) copy-start(s32[3,256]{1,0:T(4,128)} %param.10) | copy-start | bytes 9220
  57.9 19.3 %copy-start.1 = (s32[3,512]{1,0:T(4,128)S(1)}, s32[3,512]{1,0:T(4,128)}, u32[]{:S(2)}) copy-start(s32[3,512]{1,0:T(4,128)} %param.11) | copy-start | bytes 18436
  70.8 29.5 %all-to-all-start.2 = ((bf16[128,2,1024]{2,1,0:T(2,128)(2,1)}), bf16[128,2,1024]{2,1,0:T(2,128)(2,1)S(1)}, u32[]{:S(2)}, u32[]{:S(2)}) async-start(bf16[128,2,1024]{2,1,0:T(2,128)(2,1)} %reshape.662), calls=%async_computation.2 | async-start | bytes 1048576 | tf_op jit(solution)/shard_map/all_to_all | solution.py:89
